TPU v7x, 256 devices: a whole 4x4x8 slice. The times are simulated.
256 devices in a mesh: row: 64 (over z, y, core), col: 4 (over x).
Axes of the slice: x: 4, y: 4, z: 8, core: 2. Of those that a mesh axis runs over, the one named last changes fastest.
Arguments:
- node_feat: bfloat16 [131072, 50], P(('row', 'col'))
- w_one: float32 [50, 2048], replicated
- w_two: float32 [2048, 121], replicated
- send_rows: int32 [1024, 8], P(('row', 'col'))
- edge_src: int32 [131072, 12], P(('row', 'col'))
- edge_wt: float32 [131072, 12], P(('row', 'col'))
- labels: int32 [131072], P(('row', 'col'))
- label_mask: int32 [131072], P(('row', 'col'))
Outputs:
- output 1: float32 [], replicated
- output 2: float32 [50, 2048], replicated
- output 3: float32 [2048, 121], replicated
All inputs are finite; a program needn't handle non-finite values.
Results may differ from a plain program's by a relative error of at most 0.001.
Values are sent between devices in bfloat16 or wider.
A program may use at most 768 MiB of HBM per device.

v0:
```python
import jax
import jax.numpy as jnp
from jax import lax
from jax.sharding import PartitionSpec as P

PEERS = 4


def shift_perm(size, offset):
    return [(src_dev, (src_dev + offset) % size) for src_dev in range(size)]


def exchange(table, send_rows, n_rows, n_cols):
    outgoing = table[send_rows]
    from_left = lax.ppermute(outgoing[1], 'col', shift_perm(n_cols, 1))
    from_right = lax.ppermute(outgoing[0], 'col', shift_perm(n_cols, -1))
    from_above = lax.ppermute(outgoing[3], 'row', shift_perm(n_rows, 1))
    from_below = lax.ppermute(outgoing[2], 'row', shift_perm(n_rows, -1))
    return jnp.concatenate([table, from_left, from_right, from_above, from_below], axis=0)


def return_grads(halo_grad, n_rows, n_cols):
    for_list0 = lax.ppermute(halo_grad[1], 'col', shift_perm(n_cols, 1))
    for_list1 = lax.ppermute(halo_grad[0], 'col', shift_perm(n_cols, -1))
    for_list2 = lax.ppermute(halo_grad[3], 'row', shift_perm(n_rows, 1))
    for_list3 = lax.ppermute(halo_grad[2], 'row', shift_perm(n_rows, -1))
    return jnp.stack([for_list0, for_list1, for_list2, for_list3])


def aggregate(ext_table, src_cols, wt_cols):
    def add_edge(edge_k, total):
        return total + wt_cols[edge_k][:, None] * ext_table[src_cols[edge_k]].astype(jnp.float32)
    start_acc = jnp.zeros((src_cols.shape[1], ext_table.shape[1]), jnp.float32)
    return lax.fori_loop(0, src_cols.shape[0], add_edge, start_acc)


def scatter_back(grad, src_cols, wt_cols, ext_rows):
    def add_edge(edge_k, total):
        return total.at[src_cols[edge_k]].add(wt_cols[edge_k][:, None] * grad)
    start_acc = jnp.zeros((ext_rows, grad.shape[1]), jnp.float32)
    return lax.fori_loop(0, src_cols.shape[0], add_edge, start_acc)


def solution(mesh):
    n_rows = mesh.shape['row']
    n_cols = mesh.shape['col']
    grid_axes = ('row', 'col')

    def device_step(node_feat, w_one, w_two, send_rows, edge_src, edge_wt, labels, label_mask):
        n_local = node_feat.shape[0]
        src_cols = edge_src.T
        wt_cols = edge_wt.T
        w_one_b = w_one.astype(jnp.bfloat16)
        w_two_b = w_two.astype(jnp.bfloat16)
        ext_one = exchange(node_feat, send_rows, n_rows, n_cols)
        z_one = aggregate(ext_one, src_cols, wt_cols).astype(jnp.bfloat16)
        h_one = jnp.maximum(jnp.dot(z_one, w_one_b, preferred_element_type=jnp.float32), 0.0).astype(jnp.bfloat16)
        ext_two = exchange(h_one, send_rows, n_rows, n_cols)
        z_two = aggregate(ext_two, src_cols, wt_cols).astype(jnp.bfloat16)
        logits = jnp.dot(z_two, w_two_b, preferred_element_type=jnp.float32)
        weight = label_mask.astype(jnp.float32)
        label_count = lax.psum(jnp.sum(weight), grid_axes)
        log_norm = jax.nn.logsumexp(logits, axis=1)
        picked = jnp.take_along_axis(logits, labels[:, None], axis=1)[:, 0]
        mean_loss = lax.psum(jnp.sum(weight * (log_norm - picked)), grid_axes) / label_count
        class_prob = jnp.exp(logits - log_norm[:, None])
        onehot = (jnp.arange(logits.shape[1])[None, :] == labels[:, None]).astype(jnp.float32)
        d_logits = ((class_prob - onehot) * (weight / label_count)[:, None]).astype(jnp.bfloat16)
        grad_two = lax.psum(jnp.einsum('nf,nc->fc', z_two, d_logits, preferred_element_type=jnp.float32), grid_axes)
        d_z_two = jnp.einsum('nc,fc->nf', d_logits, w_two_b, preferred_element_type=jnp.float32)
        d_ext = scatter_back(d_z_two, src_cols, wt_cols, ext_two.shape[0])
        feat_width = d_ext.shape[1]
        halo_grad = d_ext[n_local:].reshape(PEERS, -1, feat_width)
        returned = return_grads(halo_grad, n_rows, n_cols)
        d_h_one = d_ext[:n_local].at[send_rows.reshape(-1)].add(returned.reshape(-1, feat_width))
        d_y_one = jnp.where(h_one > 0, d_h_one, 0.0).astype(jnp.bfloat16)
        grad_one = lax.psum(jnp.einsum('nf,ng->fg', z_one, d_y_one, preferred_element_type=jnp.float32), grid_axes)
        return mean_loss, grad_one, grad_two

    rows_spec = P(grid_axes, None)
    vec_spec = P(grid_axes)
    return jax.shard_map(device_step, mesh=mesh,
                         in_specs=(rows_spec, P(), P(), rows_spec, rows_spec, rows_spec, vec_spec, vec_spec),
                         out_specs=(P(), P(), P()), check_vma=False)
```

profile of v0, /device:TPU:1, one launch (start us, length us, event | category | flops | bytes accessed | tf_op | source)
XLA Modules:
  0.0 753.2 jit_solution(15218382341688103182)
XLA Ops:
  9.6 3.3 collective-permute-start.3
  19.6 35.8 %while.42 = (s32[]{:T(128)}, f32[512,50]{1,0:T(8,128)S(1)}, f32[12,512]{1,0:T(8,128)}, s32[12,512]{1,0:T(8,128)}, bf16[544,50]{1,0:T(8,128)(2,1)S(1)}, /*index=5*/s32[]{:T(128)}, s32[]{:T(128)}) while((s32[]{:T(128)}, f32[512,50]{1,0:T(8,128)S(1)}, f32[12,512]{1,0:T(8,128)}, s32[12,512]{1,0:T(8,128)}, ...), condition=%wide.region_1.0_spmd.clone, body=%wide.region_0.0_spmd.clone.sunk | while | flops 104963 | bytes 376935 | solution.py:34
  61.3 6.0 collective-permute-start.7
  71.5 121.7 %while.43 = (s32[]{:T(128)}, f32[512,2048]{1,0:T(8,128)}, f32[12,512]{1,0:T(8,128)}, s32[12,512]{1,0:T(8,128)}, bf16[544,2048]{1,0:T(8,128)(2,1)S(1)}, /*index=5*/s32[]{:T(128)}, s32[]{:T(128)}) while((s32[]{:T(128)}, f32[512,2048]{1,0:T(8,128)}, f32[12,512]{1,0:T(8,128)}, s32[12,512]{1,0:T(8,128)}, ...), condition=%wide.region_3.0_spmd.clone, body=%wide.region_2.0_spmd.clone.sunk | while | flops 4196867 | bytes 14698599 | solution.py:34
  73.1 3.3 gather_fusion.1
  76.4 4.2 select_add_fusion.5
  82.0 3.3 gather_fusion.1
  85.4 5.5 select_add_fusion.5
  92.3 3.3 gather_fusion.1
  95.6 5.5 select_add_fusion.5
  102.5 3.3 gather_fusion.1
  105.8 5.5 select_add_fusion.5
  112.8 3.3 gather_fusion.1
  116.1 5.5 select_add_fusion.5
  123.0 3.3 gather_fusion.1
  126.3 5.5 select_add_fusion.5
  133.2 3.3 gather_fusion.1
  136.6 5.5 select_add_fusion.5
  143.5 3.3 gather_fusion.1
  146.8 5.5 select_add_fusion.5
  153.7 3.3 gather_fusion.1
  157.1 5.5 select_add_fusion.5
  164.0 3.3 gather_fusion.1
  167.3 5.5 select_add_fusion.5
  174.2 3.3 gather_fusion.1
  177.5 5.5 select_add_fusion.5
  184.4 3.3 gather_fusion.1
  187.8 5.5 select_add_fusion.5
  193.2 3.1 fusion.32
  196.3 4.5 gather_fusion.4
  201.6 80.8 %all-reduce = (f32[]{:T(128)}, f32[]{:T(128)}) all-reduce(f32[]{:T(128)} %get-tuple-element.325, f32[]{:T(128)} %get-tuple-element.324), channel_id=1, replica_groups=mesh['row'=64,'col'=4] {'row','col'}, use_global_device_ids=true, to_apply=%region_7.0 | all-reduce | flops 2 | bytes 16 | tf_op jit(solution)/shard_map/psum | solution.py:65
  288.4 173.5 %while.41 = (s32[]{:T(128)}, f32[544,2048]{1,0:T(8,128)}, s32[12,512]{1,0:T(8,128)}, f32[12,512]{1,0:T(8,128)}, f32[512,2048]{1,0:T(8,128)}, /*index=5*/s32[]{:T(128)}) while((s32[]{:T(128)}, f32[544,2048]{1,0:T(8,128)}, s32[12,512]{1,0:T(8,128)}, f32[12,512]{1,0:T(8,128)}, f32[512,2048]{1,0:T(8,128)}, /*index=5*/s32[]{:T(128)}) %tuple.117), condition=%wide.region_12.13_spmd, body=%wide.region_10.0_spmd.sunk | while | flops 2098690 | bytes 8661077 | solution.py:41
  289.8 13.0 %scatter_custom_fusion.7 = f32[544,2048]{1,0:T(8,128)} fusion(f32[544,2048]{1,0:T(8,128)} %get-tuple-element.519, s32[512]{0:T(512)S(1)} %bitcast.55, f32[512,2048]{1,0:T(8,128)} %get-tuple-element.528, f32[512]{0:T(512)S(1)} %bitcast.48), kind=kCustom, calls=%fused_computation.7.clone.1 | custom fusion | flops 2097152 | bytes 8652800 | tf_op jit(solution)/shard_map/while/body/eval_jaxpr/scatter-add | solution.py:39
  304.3 13.0 %scatter_custom_fusion.7 = f32[544,2048]{1,0:T(8,128)} fusion(f32[544,2048]{1,0:T(8,128)} %get-tuple-element.519, s32[512]{0:T(512)S(1)} %bitcast.55, f32[512,2048]{1,0:T(8,128)} %get-tuple-element.528, f32[512]{0:T(512)S(1)} %bitcast.48), kind=kCustom, calls=%fused_computation.7.clone.1 | custom fusion | flops 2097152 | bytes 8652800 | tf_op jit(solution)/shard_map/while/body/eval_jaxpr/scatter-add | solution.py:39
  318.7 13.0 %scatter_custom_fusion.7 = f32[544,2048]{1,0:T(8,128)} fusion(f32[544,2048]{1,0:T(8,128)} %get-tuple-element.519, s32[512]{0:T(512)S(1)} %bitcast.55, f32[512,2048]{1,0:T(8,128)} %get-tuple-element.528, f32[512]{0:T(512)S(1)} %bitcast.48), kind=kCustom, calls=%fused_computation.7.clone.1 | custom fusion | flops 2097152 | bytes 8652800 | tf_op jit(solution)/shard_map/while/body/eval_jaxpr/scatter-add | solution.py:39
  333.2 13.0 %scatter_custom_fusion.7 = f32[544,2048]{1,0:T(8,128)} fusion(f32[544,2048]{1,0:T(8,128)} %get-tuple-element.519, s32[512]{0:T(512)S(1)} %bitcast.55, f32[512,2048]{1,0:T(8,128)} %get-tuple-element.528, f32[512]{0:T(512)S(1)} %bitcast.48), kind=kCustom, calls=%fused_computation.7.clone.1 | custom fusion | flops 2097152 | bytes 8652800 | tf_op jit(solution)/shard_map/while/body/eval_jaxpr/scatter-add | solution.py:39
  347.6 13.0 %scatter_custom_fusion.7 = f32[544,2048]{1,0:T(8,128)} fusion(f32[544,2048]{1,0:T(8,128)} %get-tuple-element.519, s32[512]{0:T(512)S(1)} %bitcast.55, f32[512,2048]{1,0:T(8,128)} %get-tuple-element.528, f32[512]{0:T(512)S(1)} %bitcast.48), kind=kCustom, calls=%fused_computation.7.clone.1 | custom fusion | flops 2097152 | bytes 8652800 | tf_op jit(solution)/shard_map/while/body/eval_jaxpr/scatter-add | solution.py:39
  362.1 13.0 %scatter_custom_fusion.7 = f32[544,2048]{1,0:T(8,128)} fusion(f32[544,2048]{1,0:T(8,128)} %get-tuple-element.519, s32[512]{0:T(512)S(1)} %bitcast.55, f32[512,2048]{1,0:T(8,128)} %get-tuple-element.528, f32[512]{0:T(512)S(1)} %bitcast.48), kind=kCustom, calls=%fused_computation.7.clone.1 | custom fusion | flops 2097152 | bytes 8652800 | tf_op jit(solution)/shard_map/while/body/eval_jaxpr/scatter-add | solution.py:39
  376.6 13.0 %scatter_custom_fusion.7 = f32[544,2048]{1,0:T(8,128)} fusion(f32[544,2048]{1,0:T(8,128)} %get-tuple-element.519, s32[512]{0:T(512)S(1)} %bitcast.55, f32[512,2048]{1,0:T(8,128)} %get-tuple-element.528, f32[512]{0:T(512)S(1)} %bitcast.48), kind=kCustom, calls=%fused_computation.7.clone.1 | custom fusion | flops 2097152 | bytes 8652800 | tf_op jit(solution)/shard_map/while/body/eval_jaxpr/scatter-add | solution.py:39
  391.0 13.0 %scatter_custom_fusion.7 = f32[544,2048]{1,0:T(8,128)} fusion(f32[544,2048]{1,0:T(8,128)} %get-tuple-element.519, s32[512]{0:T(512)S(1)} %bitcast.55, f32[512,2048]{1,0:T(8,128)} %get-tuple-element.528, f32[512]{0:T(512)S(1)} %bitcast.48), kind=kCustom, calls=%fused_computation.7.clone.1 | custom fusion | flops 2097152 | bytes 8652800 | tf_op jit(solution)/shard_map/while/body/eval_jaxpr/scatter-add | solution.py:39
  405.5 13.0 %scatter_custom_fusion.7 = f32[544,2048]{1,0:T(8,128)} fusion(f32[544,2048]{1,0:T(8,128)} %get-tuple-element.519, s32[512]{0:T(512)S(1)} %bitcast.55, f32[512,2048]{1,0:T(8,128)} %get-tuple-element.528, f32[512]{0:T(512)S(1)} %bitcast.48), kind=kCustom, calls=%fused_computation.7.clone.1 | custom fusion | flops 2097152 | bytes 8652800 | tf_op jit(solution)/shard_map/while/body/eval_jaxpr/scatter-add | solution.py:39
  419.9 13.0 %scatter_custom_fusion.7 = f32[544,2048]{1,0:T(8,128)} fusion(f32[544,2048]{1,0:T(8,128)} %get-tuple-element.519, s32[512]{0:T(512)S(1)} %bitcast.55, f32[512,2048]{1,0:T(8,128)} %get-tuple-element.528, f32[512]{0:T(512)S(1)} %bitcast.48), kind=kCustom, calls=%fused_computation.7.clone.1 | custom fusion | flops 2097152 | bytes 8652800 | tf_op jit(solution)/shard_map/while/body/eval_jaxpr/scatter-add | solution.py:39
  434.4 13.0 %scatter_custom_fusion.7 = f32[544,2048]{1,0:T(8,128)} fusion(f32[544,2048]{1,0:T(8,128)} %get-tuple-element.519, s32[512]{0:T(512)S(1)} %bitcast.55, f32[512,2048]{1,0:T(8,128)} %get-tuple-element.528, f32[512]{0:T(512)S(1)} %bitcast.48), kind=kCustom, calls=%fused_computation.7.clone.1 | custom fusion | flops 2097152 | bytes 8652800 | tf_op jit(solution)/shard_map/while/body/eval_jaxpr/scatter-add | solution.py:39
  448.8 13.0 %scatter_custom_fusion.7 = f32[544,2048]{1,0:T(8,128)} fusion(f32[544,2048]{1,0:T(8,128)} %get-tuple-element.519, s32[512]{0:T(512)S(1)} %bitcast.55, f32[512,2048]{1,0:T(8,128)} %get-tuple-element.528, f32[512]{0:T(512)S(1)} %bitcast.48), kind=kCustom, calls=%fused_computation.7.clone.1 | custom fusion | flops 2097152 | bytes 8652800 | tf_op jit(solution)/shard_map/while/body/eval_jaxpr/scatter-add | solution.py:39
  467.4 3.9 fusion.6
  473.6 5.2 scatter_custom_fusion.1
  478.9 3.6 fusion.3
  483.7 257.4 %all-reduce.4.cloned.1.call-done = (f32[50,2048]{1,0:T(8,128)}, f32[2048,121]{1,0:T(8,128)}) async-done(((f32[50,2048]{1,0:T(8,128)}, f32[2048,121]{1,0:T(8,128)}), (f32[50,2048]{1,0:T(8,128)}, f32[2048,121]{1,0:T(8,128)})) %all-reduce.4.cloned.1.call-update) | async-done | bytes 1400848 | tf_op jit(solution)/shard_map/psum | solution.py:77
  (192 shorter events, 108.1 us)
Async XLA Ops:
  7.2 734.0 %all-reduce.4.cloned.1.call-start = ((), (), s32[]{:S(2)}) async-start(), calls=%async_computation | async-start | bytes 3014656 | tf_op jit(solution)/shard_map/psum | solution.py:77
  9.6 10.0 %collective-permute-start.3 = (bf16[8,50]{1,0:T(8,128)(2,1)S(1)}, bf16[8,50]{1,0:T(8,128)(2,1)S(1)}, u32[]{:S(2)}, u32[]{:S(2)}) collective-permute-start(bf16[8,50]{1,0:T(8,128)(2,1)S(1)} %get-tuple-element.369), channel_id=1, source_target_pairs={{0,252},{4,0},{8,4},{12,8},{16,12},{20,16},{24,20},{28,24},{32,28}... | collective-permute-start | bytes 2408 | tf_op jit(solution)/shard_map/ppermute | solution.py:18
  12.8 6.7 collective-permute-start.2
  12.8 5.7 collective-permute-start.1
  14.9 3.6 collective-permute-start
  19.6 35.8 %copy-start.3 = (f32[50,2048]{1,0:T(8,128)S(1)}, f32[50,2048]{1,0:T(8,128)}, u32[]{:S(2)}) copy-start(f32[50,2048]{1,0:T(8,128)} %param.15) | copy-start | bytes 1228804
  60.0 10.0 %collective-permute-start.4 = (bf16[8,2048]{1,0:T(8,128)(2,1)S(1)}, bf16[8,2048]{1,0:T(8,128)(2,1)S(1)}, u32[]{:S(2)}, u32[]{:S(2)}) collective-permute-start(bf16[8,2048]{1,0:T(8,128)(2,1)S(1)} %get-tuple-element.368), channel_id=1, source_target_pairs={{0,1},{1,2},{2,3},{3,0},{4,5},{5,6},{6,7},{7,4},{8,9},{9,10},{10,1... | collective-permute-start | bytes 98312 | tf_op jit(solution)/shard_map/ppermute | solution.py:15
  61.3 10.2 %collective-permute-start.7 = (bf16[8,2048]{1,0:T(8,128)(2,1)S(1)}, bf16[8,2048]{1,0:T(8,128)(2,1)S(1)}, u32[]{:S(2)}, u32[]{:S(2)}) collective-permute-start(bf16[8,2048]{1,0:T(8,128)(2,1)S(1)} %get-tuple-element.365), channel_id=1, source_target_pairs={{0,252},{4,0},{8,4},{12,8},{16,12},{20,16},{24,20},{28,24},{32,28}... | collective-permute-start | bytes 98312 | tf_op jit(solution)/shard_map/ppermute | solution.py:18
  67.3 4.2 collective-permute-start.6
  67.3 3.8 collective-permute-start.5
  71.5 121.8 %copy-start.2 = (f32[2048,121]{1,0:T(8,128)S(1)}, f32[2048,121]{1,0:T(8,128)}, u32[]{:S(2)}) copy-start(f32[2048,121]{1,0:T(8,128)} %param.16) | copy-start | bytes 2973700
  193.2 7.7 %copy-start.4 = (s32[512]{0:T(512)S(1)}, s32[512]{0:T(512)}, u32[]{:S(2)}) copy-start(s32[512]{0:T(512)} %param.20) | copy-start | bytes 6148
  193.2 7.7 %copy-start.5 = (s32[512]{0:T(512)S(1)}, s32[512]{0:T(512)}, u32[]{:S(2)}) copy-start(s32[512]{0:T(512)} %param.21) | copy-start | bytes 6148
  461.8 9.6 %copy-start = (f32[544,2048]{1,0:T(8,128)S(1)}, f32[544,2048]{1,0:T(8,128)}, u32[]{:S(2)}) copy-start(f32[544,2048]{1,0:T(8,128)} %get-tuple-element.287) | copy-start | bytes 13369348
  462.9 10.7 %collective-permute-start.8 = (f32[8,2048]{1,0:T(8,128)S(1)}, f32[8,2048]{1,0:T(8,128)S(1)}, u32[]{:S(2)}, u32[]{:S(2)}) collective-permute-start(f32[8,2048]{1,0:T(8,128)S(1)} %get-tuple-element.361), channel_id=1, source_target_pairs={{0,1},{1,2},{2,3},{3,0},{4,5},{5,6},{6,7},{7,4},{8,9},{9,10},{10,1... | collective-permute-start | bytes 196616 | tf_op jit(solution)/shard_map/ppermute | solution.py:23
  463.0 10.6 %collective-permute-start.11 = (f32[8,2048]{1,0:T(8,128)S(1)}, f32[8,2048]{1,0:T(8,128)S(1)}, u32[]{:S(2)}, u32[]{:S(2)}) collective-permute-start(f32[8,2048]{1,0:T(8,128)S(1)} %get-tuple-element.362), channel_id=1, source_target_pairs={{0,252},{4,0},{8,4},{12,8},{16,12},{20,16},{24,20},{28,24},{32,28}... | collective-permute-start | bytes 196616 | tf_op jit(solution)/shard_map/ppermute | solution.py:26
  464.1 9.5 %collective-permute-start.10 = (f32[8,2048]{1,0:T(8,128)S(1)}, f32[8,2048]{1,0:T(8,128)S(1)}, u32[]{:S(2)}, u32[]{:S(2)}) collective-permute-start(f32[8,2048]{1,0:T(8,128)S(1)} %get-tuple-element.363), channel_id=1, source_target_pairs={{0,4},{4,8},{8,12},{12,16},{16,20},{20,24},{24,28},{28,32},{32,36}... | collective-permute-start | bytes 196616 | tf_op jit(solution)/shard_map/ppermute | solution.py:25
  464.9 8.8 %collective-permute-start.9 = (f32[8,2048]{1,0:T(8,128)S(1)}, f32[8,2048]{1,0:T(8,128)S(1)}, u32[]{:S(2)}, u32[]{:S(2)}) collective-permute-start(f32[8,2048]{1,0:T(8,128)S(1)} %get-tuple-element.364), channel_id=1, source_target_pairs={{0,3},{1,0},{2,1},{3,2},{4,7},{5,4},{6,5},{7,6},{8,11},{9,8},{10,9... | collective-permute-start | bytes 196616 | tf_op jit(solution)/shard_map/ppermute | solution.py:24
  473.6 5.3 copy-start.1
Sparse Core Ops, SparseCore 0:
  482.6 258.5 all-reduce.3
where the time goes:
time: 761 us; the launch traced here: 753 us
  waiting for transfers between devices  262 us (34%)
  other arithmetic  256 us (34%)
  local copies, waits for them, and re-layouts  102 us (13%)
  blocking collectives  80.8 us (11%)
  starting transfers between devices  19.8 us (3%)
  between operations  16.5 us (2%)
  matrix products  15.4 us (2%)
    psum x1, waiting for transfers between devices, device_step(): lax.psum(jnp.einsum('nf,ng->fg', z_one, d_y_one, preferred_element_type=j...  257 us
    scatter-add x12, other arithmetic, add_edge(): return total.at[src_cols[edge_k]].add(wt_cols[edge_k][:, None] * grad)  156 us
    psum x1, blocking collectives, device_step(): lax.psum(jnp.sum(weight * (log_norm - picked)), grid_axes) / label_count  80.8 us
    add x24, other arithmetic, add_edge(): total + wt_cols[edge_k][:, None] * ext_table[src_cols[edge_k]].astype(jnp...  65.9 us
    gather x24, local copies, waits for them, and re-layouts, add_edge(): ext_table[src_cols[edge_k]].astype(jnp.float32)  56.1 us
    select_n x24, other arithmetic, add_edge(): ext_table[src_cols[edge_k]].astype(jnp.float32)  17.6 us
    dynamic_slice x24, local copies, waits for them, and re-layouts, add_edge(): wt_cols[edge_k][:, None] * ext_table[src_cols[edge_k]].astype(jnp.float32)  17.3 us
  transfers between devices with their start and end apart: 13, of which 5 were waited for; matrix products, arithmetic and copies ran while one was open for 1% of the time, Pallas kernels for 0%

commit v1 on v0

v1 whole, which is shorter than its diff:
```python
import functools

import jax
import jax.numpy as jnp
from jax import lax
from jax.experimental import pallas as pl
from jax.experimental.pallas import tpu as pltpu
from jax.sharding import PartitionSpec as P

F32 = jnp.float32
BF16 = jnp.bfloat16
MESH = pl.DeviceIdType.MESH
LANES = 128
PEERS = 4


def mm(a, b, ca, cb):
    return lax.dot_general(a, b, (((ca,), (cb,)), ((), ())), preferred_element_type=F32)


def split3(v):
    hi = v.astype(BF16)
    rest = v - hi.astype(F32)
    mid = rest.astype(BF16)
    low = (rest - mid.astype(F32)).astype(BF16)
    return hi, mid, low


class Grid:
    def __init__(self, dims):
        self.nx, self.ny, self.nz, self.nc = dims
        self.row = lax.axis_index('row')
        self.x = lax.axis_index('col')
        self.c = lax.rem(self.row, self.nc)
        self.y = lax.rem(self.row // self.nc, self.ny)
        self.z = self.row // (self.nc * self.ny)
        self.n_rows = self.nz * self.ny * self.nc

    def size(self, axis):
        return {'x': self.nx, 'y': self.ny, 'z': self.nz, 'c': self.nc}[axis]

    def pos(self, axis):
        return getattr(self, axis)

    def plus(self, axis, d):
        n = self.size(axis)
        return lax.rem(self.pos(axis) + d, n)

    def dev(self, axis, d):
        at = {'x': self.x, 'y': self.y, 'z': self.z, 'c': self.c}
        at[axis] = self.plus(axis, d)
        return ((at['z'] * self.ny + at['y']) * self.nc + at['c'], at['x'])

    def peer(self, p):
        if p == 0:
            return (self.row, lax.rem(self.x + self.nx - 1, self.nx))
        if p == 1:
            return (self.row, lax.rem(self.x + 1, self.nx))
        if p == 2:
            return (lax.rem(self.row + self.n_rows - 1, self.n_rows), self.x)
        return (lax.rem(self.row + 1, self.n_rows), self.x)


class Stream:
    def __init__(self, g, refs, rows):
        (self.b, self.rc, self.h, self.r1, self.p, self.r2, self.q, self.rz,
         self.f, self.ssem, self.rsem) = refs
        self.g, self.rows = g, rows
        self.n_sem = 0
        self.sent = []

    def copy(self, src, dst, dev):
        k = self.n_sem
        self.n_sem += 1
        op = pltpu.make_async_remote_copy(src_ref=src, dst_ref=dst, send_sem=self.ssem.at[k],
                                          recv_sem=self.rsem.at[k], device_id=dev, device_id_type=MESH)
        op.start()
        self.sent.append(op)
        return op

    def steps(self):
        g, rows = self.g, self.rows
        half, quarter = rows // 2, rows // 4
        ds = lambda start, size: pl.ds(pl.multiple_of(start, size), size)
        orders = (('x', 'y'), ('y', 'x'))
        other = g.plus('c', 1)
        op = self.copy(self.b.at[ds(other * half, half)], self.rc, g.dev('c', 1))
        yield
        op.wait_recv()
        self.h[...] = self.b[ds(g.c * half, half)] + self.rc[...]
        n1 = quarter // g.nx
        ops = []
        for col, (a1, a2) in enumerate(orders):
            for d in range(1, g.size(a1)):
                ops.append(self.copy(self.h.at[ds(col * quarter + g.plus(a1, d) * n1, n1)],
                                     self.r1.at[col, d - 1], g.dev(a1, d)))
        yield
        for op in ops:
            op.wait_recv()
        for col, (a1, a2) in enumerate(orders):
            total = self.h[ds(col * quarter + g.pos(a1) * n1, n1)]
            for d in range(1, g.size(a1)):
                total = total + self.r1[col, d - 1]
            self.p[col] = total
        n2 = n1 // g.ny
        ops = []
        for col, (a1, a2) in enumerate(orders):
            for d in range(1, g.size(a2)):
                ops.append(self.copy(self.p.at[col, ds(g.plus(a2, d) * n2, n2)],
                                     self.r2.at[col, d - 1], g.dev(a2, d)))
        yield
        for op in ops:
            op.wait_recv()
        for col, (a1, a2) in enumerate(orders):
            total = self.p[col, ds(g.pos(a2) * n2, n2)]
            for d in range(1, g.size(a2)):
                total = total + self.r2[col, d - 1]
            self.q[pl.ds(col * n2, n2)] = total
        n3 = 2 * n2 // g.nz
        ops = []
        for d in range(1, g.nz):
            ops.append(self.copy(self.q.at[ds(g.plus('z', d) * n3, n3)], self.rz.at[d - 1], g.dev('z', d)))
        yield
        for op in ops:
            op.wait_recv()
        total = self.q[ds(g.z * n3, n3)]
        for d in range(1, g.nz):
            total = total + self.rz[d - 1]
        base1 = [g.c * half + col * quarter for col in range(2)]
        base2 = [base1[0] + g.x * n1, base1[1] + g.y * n1]
        base3 = [base2[0] + g.y * n2, base2[1] + g.x * n2]
        per_col = g.nz // 2
        which = g.z // per_col
        start = base3[0] * (1 - which) + base3[1] * which + lax.rem(g.z, per_col) * n3
        self.f[ds(start, n3)] = total
        ops = []
        for d in range(1, g.nz):
            ops.append(self.copy(self.f.at[ds(start, n3)], self.f.at[ds(start, n3)], g.dev('z', d)))
        yield
        for op in ops:
            op.wait_recv()
        ops = []
        for col, (a1, a2) in enumerate(orders):
            for d in range(1, g.size(a2)):
                part = self.f.at[ds(base3[col], n2)]
                ops.append(self.copy(part, part, g.dev(a2, d)))
        yield
        for op in ops:
            op.wait_recv()
        ops = []
        for col, (a1, a2) in enumerate(orders):
            for d in range(1, g.size(a1)):
                part = self.f.at[ds(base2[col], n1)]
                ops.append(self.copy(part, part, g.dev(a1, d)))
        yield
        for op in ops:
            op.wait_recv()
        part = self.f.at[ds(g.c * half, half)]
        op = self.copy(part, part, g.dev('c', 1))
        yield
        op.wait_recv()
        for op in self.sent:
            op.wait_send()


def step_kernel(dims, feat_in, classes, feat_ref, w1_ref, w2_ref, send_ref, src_ref, wt_ref, lab_ref, mask_ref,
                loss_ref, g1_ref, g2_ref, *scratch):
    (at, fp, w1p, w2p, sel, z1t, z1tb, h1t, h1h, z2t, d1t, ptc,
     hs, hr, hs_sem, hr_sem, mb, mr, ms_sem, mr_sem) = scratch[:20]
    refs2, refs1 = scratch[20:31], scratch[31:42]
    g = Grid(dims)
    n = feat_ref.shape[1]
    hid = w1_ref.shape[1]
    halo = send_ref.shape[0] * send_ref.shape[1]
    per = send_ref.shape[1]
    deg = src_ref.shape[0]
    ext = n + halo

    barrier = pltpu.get_barrier_semaphore()
    greet = [g.dev('c', 1)]
    for axis in ('x', 'y', 'z'):
        greet += [g.dev(axis, d) for d in range(1, g.size(axis))]
    far = lax.rem(g.row + g.n_rows + 2 * g.c - 1, g.n_rows)
    greet.append((far, g.x))
    for dev in greet:
        pl.semaphore_signal(barrier, inc=1, device_id=dev, device_id_type=MESH)

    weight = mask_ref[...].astype(F32)
    mb[0] = jnp.full(mb.shape[1:], 1.0, F32) * jnp.sum(weight)

    def build(i, carry):
        first = pl.multiple_of(i * 16, 16)
        ids = first + lax.broadcasted_iota(jnp.int32, (16, n), 0)
        total = jnp.zeros((16, n), F32)
        for k in range(deg):
            total = total + jnp.where(src_ref[k:k + 1, :] == ids, wt_ref[k:k + 1, :], 0.0)
        parts = split3(total)
        for j in range(3):
            at[j, pl.ds(first, 16), :] = parts[j]
        return carry

    lax.fori_loop(0, ext // 16, build, 0)

    eye = lax.broadcasted_iota(jnp.int32, (per, per), 0) == lax.broadcasted_iota(jnp.int32, (per, per), 1)
    lane_ids = lax.broadcasted_iota(jnp.int32, (per, n), 1)
    picks = []
    for p in range(PEERS):
        rows = jnp.broadcast_to(send_ref[p:p + 1, :], (per, per))
        column = jnp.sum(jnp.where(eye, rows, 0), axis=1, keepdims=True)
        picks.append((column == lane_ids).astype(F32))
    sel[...] = jnp.concatenate(picks, axis=0).astype(BF16)

    fp[...] = jnp.concatenate([feat_ref[...].astype(F32), jnp.zeros((LANES - feat_in, n), F32)], axis=0).astype(BF16)
    w1p[...] = jnp.concatenate([w1_ref[...], jnp.zeros((w1p.shape[0] - feat_in, hid), F32)], axis=0).astype(BF16)
    w2p[...] = jnp.concatenate([w2_ref[...], jnp.zeros((hid, LANES - classes), F32)], axis=1).astype(BF16)

    pl.semaphore_wait(barrier, len(greet))

    def exchange(stage, rows):
        hs[stage] = rows
        ops = []
        for p in range(PEERS):
            ops.append(pltpu.make_async_remote_copy(
                src_ref=hs.at[stage, pl.ds(p * per, per)], dst_ref=hr.at[stage, pl.ds((p ^ 1) * per, per)],
                send_sem=hs_sem.at[stage, p], recv_sem=hr_sem.at[stage, p ^ 1],
                device_id=g.peer(p), device_id_type=MESH))
            ops[-1].start()
        return ops

    def arrived(ops):
        for op in ops:
            op.wait()

    def count_steps():
        k = 0
        for stage, axis in enumerate(('c', 'x', 'y', 'z')):
            ops = []
            for d in range(1, g.size(axis)):
                ops.append(pltpu.make_async_remote_copy(
                    src_ref=mb.at[stage], dst_ref=mr.at[k], send_sem=ms_sem.at[k], recv_sem=mr_sem.at[k],
                    device_id=g.dev(axis, d), device_id_type=MESH))
                ops[-1].start()
                k += 1
            yield
            arrived(ops)
            total = mb[stage]
            for j in range(k - len(ops), k):
                total = total + mr[j]
            mb[stage + 1] = total

    count = count_steps()
    ops = exchange(0, mm(sel[...], fp[...], 1, 1))
    next(count)

    z1 = mm(fp[...], at[0, 0:n, :], 1, 0) + mm(fp[...], at[1, 0:n, :], 1, 0) + mm(fp[...], at[2, 0:n, :], 1, 0)
    arrived(ops)
    fh = hr[0].astype(BF16)
    z1 = z1 + (mm(fh, at[0, n:ext, :], 0, 0) + mm(fh, at[1, n:ext, :], 0, 0) + mm(fh, at[2, n:ext, :], 0, 0))
    z1t[...] = z1.astype(BF16)
    ops = exchange(1, mm(sel[...], z1t[...], 1, 1))
    next(count)
    kf = w1p.shape[0]
    chunk = min(hid, 512)
    n_chunks = hid // chunk
    for i in range(n_chunks):
        s = slice(i * chunk, (i + 1) * chunk)
        h1t[s, :] = jnp.maximum(mm(w1p[:, s], z1t[0:kf, :], 0, 0), 0.0).astype(BF16)
    next(count)
    z1tb[0:LANES // 2, :] = jnp.zeros((LANES // 2, n), BF16)
    z1tb[LANES // 2:, :] = z1t[0:LANES // 2, :]

    def own_part(i):
        s = slice(i * chunk, (i + 1) * chunk)
        return mm(h1t[s, :], at[0, 0:n, :], 1, 0) + mm(h1t[s, :], at[1, 0:n, :], 1, 0) + mm(h1t[s, :], at[2, 0:n, :], 1, 0)

    first_part = own_part(0)
    arrived(ops)
    z1h = hr[1][:, 0:kf].astype(BF16)
    for i in range(n_chunks):
        s = slice(i * chunk, (i + 1) * chunk)
        h1h[s, :] = jnp.maximum(mm(w1p[:, s], z1h, 0, 1), 0.0).astype(BF16)
    logits = jnp.zeros((LANES, n), F32)
    for i in range(n_chunks):
        s = slice(i * chunk, (i + 1) * chunk)
        part = first_part if i == 0 else own_part(i)
        hh = h1h[s, :]
        part = part + (mm(hh, at[0, n:ext, :], 1, 0) + mm(hh, at[1, n:ext, :], 1, 0) + mm(hh, at[2, n:ext, :], 1, 0))
        z2 = part.astype(BF16)
        z2t[s, :] = z2
        logits = logits + mm(w2p[s, :], z2, 0, 0)
        if i == n_chunks // 2:
            next(count)
    for _ in count:
        pass

    label_count = mb[4, 0:1, 0:1]
    ids = lax.broadcasted_iota(jnp.int32, (LANES, n), 0)
    valid = ids < classes
    top = jnp.max(jnp.where(valid, logits, -jnp.inf), axis=0, keepdims=True)
    log_norm = jnp.log(jnp.sum(jnp.where(valid, jnp.exp(logits - top), 0.0), axis=0, keepdims=True)) + top
    onehot = ids == lab_ref[...]
    picked = jnp.sum(jnp.where(onehot, logits, 0.0), axis=0, keepdims=True)
    loss = jnp.sum(weight * (log_norm - picked))
    prob = jnp.exp(logits - log_norm)
    scale = weight / label_count
    gt = jnp.where(valid, (prob - onehot.astype(F32)) * scale, 0.0).astype(BF16)

    ops = exchange(2, mm(at[0, n:ext, :], gt, 1, 1) + mm(at[1, n:ext, :], gt, 1, 1) + mm(at[2, n:ext, :], gt, 1, 1))

    b2 = refs2[0]
    lane = lax.broadcasted_iota(jnp.int32, (chunk, LANES), 1)
    for i in range(n_chunks):
        s = slice(i * chunk, (i + 1) * chunk)
        b2[s, :] = jnp.where(lane == classes, loss, mm(z2t[s, :], gt, 1, 1))
    stream2 = Stream(g, refs2, hid).steps()
    next(stream2)

    pt = mm(gt, at[0, 0:n, :], 1, 1) + mm(gt, at[1, 0:n, :], 1, 1) + mm(gt, at[2, 0:n, :], 1, 1)
    arrived(ops)
    for part in split3(hr[2]):
        pt = pt + mm(part, sel[...], 0, 0)
    for j, part in enumerate(split3(pt)):
        ptc[j] = part
    next(stream2)
    for i in range(n_chunks):
        s = slice(i * chunk, (i + 1) * chunk)
        dh = mm(w2p[s, :], ptc[0], 1, 0) + mm(w2p[s, :], ptc[1], 1, 0) + mm(w2p[s, :], ptc[2], 1, 0)
        d1t[s, :] = jnp.where(h1t[s, :].astype(F32) > 0.0, dh, 0.0).astype(BF16)
    next(stream2)
    b1 = refs1[0]
    half = hid // 2
    b1[...] = mm(d1t[0:half, :], z1t[...], 1, 1) + mm(d1t[half:hid, :], z1tb[...], 1, 1)
    stream1 = Stream(g, refs1, half).steps()
    next(stream1)
    active = [stream2, stream1]
    while active:
        for stream in list(active):
            if next(stream, 'end') == 'end':
                active.remove(stream)

    f2, f1 = refs2[8], refs1[8]
    loss_ref[...] = f2[0:1, classes:classes + 1] / label_count
    g2_ref[...] = f2[:, 0:classes]
    flip = jnp.transpose(f1[...])
    g1_ref[:, 0:half] = flip[0:feat_in, :]
    g1_ref[:, half:hid] = flip[LANES // 2:LANES // 2 + feat_in, :]


def stream_scratch(rows, dims):
    nx, ny, nz, nc = dims
    half, quarter = rows // 2, rows // 4
    n1 = quarter // nx
    n2 = n1 // ny
    n3 = 2 * n2 // nz
    copies = 2 + 4 * (nx - 1) + 4 * (ny - 1) + 2 * (nz - 1)
    return [
        pltpu.VMEM((rows, LANES), F32), pltpu.VMEM((half, LANES), F32), pltpu.VMEM((half, LANES), F32),
        pltpu.VMEM((2, nx - 1, n1, LANES), F32), pltpu.VMEM((2, n1, LANES), F32),
        pltpu.VMEM((2, ny - 1, n2, LANES), F32), pltpu.VMEM((2 * n2, LANES), F32),
        pltpu.VMEM((nz - 1, n3, LANES), F32), pltpu.VMEM((rows, LANES), F32),
        pltpu.SemaphoreType.DMA((copies,)), pltpu.SemaphoreType.DMA((copies,))]


def make_step(dims):
    def device_step(node_feat, w_one, w_two, send_rows, edge_src, edge_wt, labels, label_mask):
        n, feat_in = node_feat.shape
        hid, classes = w_two.shape
        halo = send_rows.size
        ext = n + halo
        nx, ny, nz, nc = dims
        n_count = nx + ny + nz + nc - 4
        kf = 64
        scratch = [
            pltpu.VMEM((3, ext, n), BF16), pltpu.VMEM((LANES, n), BF16), pltpu.VMEM((kf, hid), BF16), pltpu.VMEM((hid, LANES), BF16),
            pltpu.VMEM((halo, n), BF16), pltpu.VMEM((LANES, n), BF16), pltpu.VMEM((LANES, n), BF16),
            pltpu.VMEM((hid, n), BF16), pltpu.VMEM((hid, halo), BF16), pltpu.VMEM((hid, n), BF16),
            pltpu.VMEM((hid, n), BF16), pltpu.VMEM((3, LANES, n), BF16),
            pltpu.VMEM((3, halo, LANES), F32), pltpu.VMEM((3, halo, LANES), F32),
            pltpu.SemaphoreType.DMA((3, PEERS)), pltpu.SemaphoreType.DMA((3, PEERS)),
            pltpu.VMEM((5, 8, LANES), F32), pltpu.VMEM((n_count, 8, LANES), F32),
            pltpu.SemaphoreType.DMA((n_count,)), pltpu.SemaphoreType.DMA((n_count,)),
        ] + stream_scratch(hid, dims) + stream_scratch(hid // 2, dims)
        vmem = pl.BlockSpec(memory_space=pltpu.VMEM)
        loss, grad_one, grad_two = pl.pallas_call(
            functools.partial(step_kernel, dims, feat_in, classes),
            out_shape=(jax.ShapeDtypeStruct((1, 1), F32), jax.ShapeDtypeStruct((feat_in, hid), F32),
                       jax.ShapeDtypeStruct((hid, classes), F32)),
            in_specs=[vmem] * 8, out_specs=(vmem,) * 3, scratch_shapes=scratch,
            compiler_params=pltpu.CompilerParams(collective_id=0, has_side_effects=True,
                                                 vmem_limit_bytes=60 * 1024 * 1024),
        )(node_feat.T, w_one, w_two, send_rows, edge_src.T, edge_wt.T, labels.reshape(1, n), label_mask.reshape(1, n))
        return loss[0, 0], grad_one, grad_two
    return device_step


def build(mesh, dims):
    grid_axes = ('row', 'col')
    rows_spec = P(grid_axes, None)
    vec_spec = P(grid_axes)
    return jax.shard_map(make_step(dims), mesh=mesh,
                         in_specs=(rows_spec, P(), P(), rows_spec, rows_spec, rows_spec, vec_spec, vec_spec),
                         out_specs=(P(), P(), P()), check_vma=False)


def solution(mesh):
    nx, ny, nc = mesh.shape['col'], 4, 2
    return build(mesh, (nx, ny, mesh.shape['row'] // (ny * nc), nc))
```

time: 761 us -> 79.9 us (0.10)
  waiting for transfers between devices: 262 us -> 0 us
  other arithmetic: 256 us -> 0 us
  local copies, waits for them, and re-layouts: 102 us -> 4.08 us
  blocking collectives: 80.8 us -> 0 us
  Pallas kernels: 0 us -> 73.2 us
  starting transfers between devices: 19.8 us -> 0 us
  matrix products: 15.4 us -> 0 us
  between operations: 16.5 us -> 2.41 us
    psum x1 -> x0, waiting for transfers between devices: 257 us -> none  [device_step(): lax.psum(jnp.einsum('nf,ng->fg', z_one, d_y_one, preferred_element_type=j...]
    scatter-add x13 -> x0, other arithmetic: 161 us -> none  [the longest x12 156 us: add_edge(): return total.at[src_cols[edge_k]].add(wt_cols[edge_k][:, None] * grad)]
    psum x1 -> x0, blocking collectives: 80.8 us -> none  [device_step(): lax.psum(jnp.sum(weight * (log_norm - picked)), grid_axes) / label_count]
    pallas_call x0 -> x1, Pallas kernels: none -> 73.2 us  [device_step(): pl.pallas_call(functools.partial(step_kernel, dims, feat_in, classes), ou...]
    add x24 -> x0, other arithmetic: 65.9 us -> none  [add_edge(): total + wt_cols[edge_k][:, None] * ext_table[src_cols[edge_k]].astype(jnp...]
    gather x27 -> x0, local copies, waits for them, and re-layouts: 63.9 us -> none  [the longest x24 56.1 us: add_edge(): ext_table[src_cols[edge_k]].astype(jnp.float32)]
    select_n x40 -> x0, other arithmetic: 27.6 us -> none  [the longest x24 17.6 us: add_edge(): ext_table[src_cols[edge_k]].astype(jnp.float32)]
    dynamic_slice x36 -> x0, local copies, waits for them, and re-layouts: 26 us -> none  [the longest x24 17.3 us: add_edge(): wt_cols[edge_k][:, None] * ext_table[src_cols[edge_k]].astype(jnp.float32)]
  transfers between devices with their start and end apart: 13 -> 0, of which waited for: 5 -> 0; matrix products, arithmetic and copies ran while one was open for 1% -> 0% of each run, Pallas kernels for 0% -> 0%
where the time goes in v1:
time: 79.9 us; the launch traced here: 79.7 us
  Pallas kernels  73.2 us (92%)
  local copies, waits for them, and re-layouts  4.08 us (5%)
  between operations  2.41 us (3%)
    pallas_call x1, Pallas kernels, device_step(): pl.pallas_call(functools.partial(step_kernel, dims, feat_in, classes), ou...  73.2 us
    unnamed x2, local copies, waits for them, and re-layouts  4.08 us

profile of v1, /device:TPU:1, one launch (start us, length us, event | category | flops | bytes accessed | tf_op | source)
XLA Modules:
  0.0 79.7 jit_solution(14511001569264640113)
XLA Ops:
  0.6 73.2 %shard_map.103 = (f32[1,1]{1,0:T(1,128)}, f32[50,2048]{1,0:T(8,128)}, f32[2048,121]{1,0:T(8,128)}) custom-call(bf16[50,512]{1,0:T(8,128)(2,1)} %bitcast.6, f32[50,2048]{1,0:T(8,128)} %w1_ref.1, f32[2048,121]{1,0:T(8,128)} %w2_ref.1, s32[4,8]{1,0:T(4,128)} %send_ref.1, s32[12,512]{1,0:T(8,128)} %bitcast.7, f32[12,512]{1,0:T(8,128)} %bitcast.8, ...), custom_call_target="tpu_custom_call" | custom-call | tf_op jit(solution)/shard_map/pallas_call | solution.py:384
  74.5 1.8 %copy.15 = f32[50,2048]{1,0:T(8,128)} copy(f32[50,2048]{1,0:T(8,128)} %get-tuple-element.13) | data formatting | bytes 819200
  76.3 2.3 %copy.16 = f32[2048,121]{1,0:T(8,128)} copy(f32[2048,121]{1,0:T(8,128)} %get-tuple-element.14) | data formatting | bytes 1982464

commit v2 on v1

--- a/solution.py
+++ b/solution.py
@@ -163,11 +163,13 @@
             op.wait_send()
 
 
-def step_kernel(dims, feat_in, classes, feat_ref, w1_ref, w2_ref, send_ref, src_ref, wt_ref, lab_ref, mask_ref,
+def step_kernel(dims, feat_in, classes, feat_hbm, w1_hbm, w2_hbm, send_hbm, src_hbm, wt_hbm, lab_hbm, mask_hbm,
                 loss_ref, g1_ref, g2_ref, *scratch):
-    (at, fp, w1p, w2p, sel, z1t, z1tb, h1t, h1h, z2t, d1t, ptc,
-     hs, hr, hs_sem, hr_sem, mb, mr, ms_sem, mr_sem) = scratch[:20]
-    refs2, refs1 = scratch[20:31], scratch[31:42]
+    (feat_ref, w1_ref, w2_ref, send_ref, src_ref, wt_ref, lab_ref, mask_ref, in_sem,
+     at, ath, fp, w1p, w2p, sel, z1t, z1tb, h1t, h1h, z2own, z2t, d1t, ptc,
+     hs, hr, hs_sem, hr_sem, mb, mr, ms_sem, mr_sem, seen) = scratch[:32]
+    refs2, refs1 = scratch[32:43], scratch[43:54]
+    scope = jax.named_scope
     g = Grid(dims)
     n = feat_ref.shape[1]
     hid = w1_ref.shape[1]
@@ -178,43 +180,46 @@
 
     barrier = pltpu.get_barrier_semaphore()
     greet = [g.dev('c', 1)]
-    for axis in ('x', 'y', 'z'):
+    for axis in ('x', 'y'):
         greet += [g.dev(axis, d) for d in range(1, g.size(axis))]
+    beside = [g.dev('z', d) for d in sorted({1, g.nz - 1})]
+    greet += beside
     far = lax.rem(g.row + g.n_rows + 2 * g.c - 1, g.n_rows)
     greet.append((far, g.x))
     for dev in greet:
         pl.semaphore_signal(barrier, inc=1, device_id=dev, device_id_type=MESH)
 
-    weight = mask_ref[...].astype(F32)
-    mb[0] = jnp.full(mb.shape[1:], 1.0, F32) * jnp.sum(weight)
-
-    def build(i, carry):
-        first = pl.multiple_of(i * 16, 16)
-        ids = first + lax.broadcasted_iota(jnp.int32, (16, n), 0)
-        total = jnp.zeros((16, n), F32)
-        for k in range(deg):
-            total = total + jnp.where(src_ref[k:k + 1, :] == ids, wt_ref[k:k + 1, :], 0.0)
-        parts = split3(total)
+    loads = {}
+    for k, (name, src, dst) in enumerate((
+            ('send', send_hbm, send_ref), ('feat', feat_hbm, feat_ref), ('mask', mask_hbm, mask_ref),
+            ('src', src_hbm, src_ref), ('wt', wt_hbm, wt_ref), ('w1', w1_hbm, w1_ref),
+            ('lab', lab_hbm, lab_ref), ('w2', w2_hbm, w2_ref))):
+        loads[name] = pltpu.make_async_copy(src, dst, in_sem.at[k])
+        loads[name].start()
+
+    def loaded(*names):
+        for name in names:
+            loads[name].wait()
+
+    with scope('prep'):
+        loaded('send', 'feat', 'mask')
+        weight = mask_ref[...].astype(F32)
+        mb[0] = jnp.full(mb.shape[1:], 1.0, F32) * jnp.sum(weight)
+        eye = lax.broadcasted_iota(jnp.int32, (per, per), 0) == lax.broadcasted_iota(jnp.int32, (per, per), 1)
+        lane_ids = lax.broadcasted_iota(jnp.int32, (per, n), 1)
+        picks = []
+        for p in range(PEERS):
+            rows = jnp.broadcast_to(send_ref[p:p + 1, :], (per, per))
+            column = jnp.sum(jnp.where(eye, rows, 0), axis=1, keepdims=True)
+            picks.append((column == lane_ids).astype(F32))
+        one_sel = jnp.concatenate(picks, axis=0).astype(BF16)
         for j in range(3):
-            at[j, pl.ds(first, 16), :] = parts[j]
-        return carry
-
-    lax.fori_loop(0, ext // 16, build, 0)
-
-    eye = lax.broadcasted_iota(jnp.int32, (per, per), 0) == lax.broadcasted_iota(jnp.int32, (per, per), 1)
-    lane_ids = lax.broadcasted_iota(jnp.int32, (per, n), 1)
-    picks = []
-    for p in range(PEERS):
-        rows = jnp.broadcast_to(send_ref[p:p + 1, :], (per, per))
-        column = jnp.sum(jnp.where(eye, rows, 0), axis=1, keepdims=True)
-        picks.append((column == lane_ids).astype(F32))
-    sel[...] = jnp.concatenate(picks, axis=0).astype(BF16)
-
-    fp[...] = jnp.concatenate([feat_ref[...].astype(F32), jnp.zeros((LANES - feat_in, n), F32)], axis=0).astype(BF16)
-    w1p[...] = jnp.concatenate([w1_ref[...], jnp.zeros((w1p.shape[0] - feat_in, hid), F32)], axis=0).astype(BF16)
-    w2p[...] = jnp.concatenate([w2_ref[...], jnp.zeros((hid, LANES - classes), F32)], axis=1).astype(BF16)
-
-    pl.semaphore_wait(barrier, len(greet))
+            sel[j * halo:(j + 1) * halo, :] = one_sel
+        fp[...] = jnp.concatenate([feat_ref[...].astype(F32), jnp.zeros((LANES - feat_in, n), F32)], axis=0).astype(BF16)
+        first_rows = mm(one_sel, fp[...], 1, 1)
+
+    with scope('barrier'):
+        pl.semaphore_wait(barrier, len(greet))
 
     def exchange(stage, rows):
         hs[stage] = rows
@@ -248,102 +253,154 @@
                 total = total + mr[j]
             mb[stage + 1] = total
 
+    def seen_steps():
+        for rnd in range(seen.shape[0]):
+            for dev in beside:
+                pl.semaphore_signal(seen.at[rnd], inc=1, device_id=dev, device_id_type=MESH)
+            yield
+            pl.semaphore_wait(seen.at[rnd], len(beside))
+
+    def three(stack):
+        return jnp.concatenate([stack, stack, stack], axis=0)
+
+    ops = exchange(0, first_rows)
     count = count_steps()
-    ops = exchange(0, mm(sel[...], fp[...], 1, 1))
     next(count)
-
-    z1 = mm(fp[...], at[0, 0:n, :], 1, 0) + mm(fp[...], at[1, 0:n, :], 1, 0) + mm(fp[...], at[2, 0:n, :], 1, 0)
-    arrived(ops)
-    fh = hr[0].astype(BF16)
-    z1 = z1 + (mm(fh, at[0, n:ext, :], 0, 0) + mm(fh, at[1, n:ext, :], 0, 0) + mm(fh, at[2, n:ext, :], 0, 0))
-    z1t[...] = z1.astype(BF16)
-    ops = exchange(1, mm(sel[...], z1t[...], 1, 1))
-    next(count)
+    rounds = seen_steps()
+    next(rounds, None)
+
+    with scope('build'):
+        loaded('src', 'wt')
+
+        def build(i, carry):
+            first = pl.multiple_of(i * 16, 16)
+            ids = first + lax.broadcasted_iota(jnp.int32, (16, n), 0)
+            total = jnp.zeros((16, n), F32)
+            for k in range(deg):
+                total = total + jnp.where(src_ref[k:k + 1, :] == ids, wt_ref[k:k + 1, :], 0.0)
+            parts = split3(total)
+            for j in range(3):
+                at[j, pl.ds(first, 16), :] = parts[j]
+            return carry
+
+        lax.fori_loop(0, ext // 16, build, 0)
+        for j in range(3):
+            ath[j * halo:(j + 1) * halo, :] = at[j, n:ext, :]
+
+    with scope('z1own'):
+        next(count)
+        next(rounds, None)
+        z1 = mm(fp[...], at[0, 0:n, :], 1, 0) + mm(fp[...], at[1, 0:n, :], 1, 0) + mm(fp[...], at[2, 0:n, :], 1, 0)
+        loaded('w1')
+        w1p[...] = jnp.concatenate([w1_ref[...], jnp.zeros((w1p.shape[0] - feat_in, hid), F32)], axis=0).astype(BF16)
+    with scope('z1wait'):
+        arrived(ops)
+    with scope('z1'):
+        z1 = z1 + mm(three(hr[0].astype(BF16)), ath[...], 0, 0)
+        z1t[...] = z1.astype(BF16)
+        ops = exchange(1, mm(sel[0:halo, :], z1t[...], 1, 1))
+        next(rounds, None)
     kf = w1p.shape[0]
     chunk = min(hid, 512)
     n_chunks = hid // chunk
-    for i in range(n_chunks):
-        s = slice(i * chunk, (i + 1) * chunk)
-        h1t[s, :] = jnp.maximum(mm(w1p[:, s], z1t[0:kf, :], 0, 0), 0.0).astype(BF16)
-    next(count)
-    z1tb[0:LANES // 2, :] = jnp.zeros((LANES // 2, n), BF16)
-    z1tb[LANES // 2:, :] = z1t[0:LANES // 2, :]
-
-    def own_part(i):
-        s = slice(i * chunk, (i + 1) * chunk)
-        return mm(h1t[s, :], at[0, 0:n, :], 1, 0) + mm(h1t[s, :], at[1, 0:n, :], 1, 0) + mm(h1t[s, :], at[2, 0:n, :], 1, 0)
-
-    first_part = own_part(0)
-    arrived(ops)
-    z1h = hr[1][:, 0:kf].astype(BF16)
-    for i in range(n_chunks):
-        s = slice(i * chunk, (i + 1) * chunk)
-        h1h[s, :] = jnp.maximum(mm(w1p[:, s], z1h, 0, 1), 0.0).astype(BF16)
-    logits = jnp.zeros((LANES, n), F32)
-    for i in range(n_chunks):
-        s = slice(i * chunk, (i + 1) * chunk)
-        part = first_part if i == 0 else own_part(i)
-        hh = h1h[s, :]
-        part = part + (mm(hh, at[0, n:ext, :], 1, 0) + mm(hh, at[1, n:ext, :], 1, 0) + mm(hh, at[2, n:ext, :], 1, 0))
-        z2 = part.astype(BF16)
-        z2t[s, :] = z2
-        logits = logits + mm(w2p[s, :], z2, 0, 0)
-        if i == n_chunks // 2:
-            next(count)
-    for _ in count:
-        pass
-
-    label_count = mb[4, 0:1, 0:1]
-    ids = lax.broadcasted_iota(jnp.int32, (LANES, n), 0)
-    valid = ids < classes
-    top = jnp.max(jnp.where(valid, logits, -jnp.inf), axis=0, keepdims=True)
-    log_norm = jnp.log(jnp.sum(jnp.where(valid, jnp.exp(logits - top), 0.0), axis=0, keepdims=True)) + top
-    onehot = ids == lab_ref[...]
-    picked = jnp.sum(jnp.where(onehot, logits, 0.0), axis=0, keepdims=True)
-    loss = jnp.sum(weight * (log_norm - picked))
-    prob = jnp.exp(logits - log_norm)
-    scale = weight / label_count
-    gt = jnp.where(valid, (prob - onehot.astype(F32)) * scale, 0.0).astype(BF16)
-
-    ops = exchange(2, mm(at[0, n:ext, :], gt, 1, 1) + mm(at[1, n:ext, :], gt, 1, 1) + mm(at[2, n:ext, :], gt, 1, 1))
-
-    b2 = refs2[0]
-    lane = lax.broadcasted_iota(jnp.int32, (chunk, LANES), 1)
-    for i in range(n_chunks):
-        s = slice(i * chunk, (i + 1) * chunk)
-        b2[s, :] = jnp.where(lane == classes, loss, mm(z2t[s, :], gt, 1, 1))
-    stream2 = Stream(g, refs2, hid).steps()
-    next(stream2)
-
-    pt = mm(gt, at[0, 0:n, :], 1, 1) + mm(gt, at[1, 0:n, :], 1, 1) + mm(gt, at[2, 0:n, :], 1, 1)
-    arrived(ops)
-    for part in split3(hr[2]):
-        pt = pt + mm(part, sel[...], 0, 0)
-    for j, part in enumerate(split3(pt)):
-        ptc[j] = part
-    next(stream2)
-    for i in range(n_chunks):
-        s = slice(i * chunk, (i + 1) * chunk)
-        dh = mm(w2p[s, :], ptc[0], 1, 0) + mm(w2p[s, :], ptc[1], 1, 0) + mm(w2p[s, :], ptc[2], 1, 0)
-        d1t[s, :] = jnp.where(h1t[s, :].astype(F32) > 0.0, dh, 0.0).astype(BF16)
-    next(stream2)
-    b1 = refs1[0]
-    half = hid // 2
-    b1[...] = mm(d1t[0:half, :], z1t[...], 1, 1) + mm(d1t[half:hid, :], z1tb[...], 1, 1)
-    stream1 = Stream(g, refs1, half).steps()
-    next(stream1)
-    active = [stream2, stream1]
+    with scope('h1'):
+        for i in range(n_chunks):
+            s = slice(i * chunk, (i + 1) * chunk)
+            h1t[s, :] = jnp.maximum(mm(w1p[:, s], z1t[0:kf, :], 0, 0), 0.0).astype(BF16)
+        z1tb[0:LANES // 2, :] = jnp.zeros((LANES // 2, n), BF16)
+        z1tb[LANES // 2:, :] = z1t[0:LANES // 2, :]
+        loaded('w2')
+        wide = jnp.concatenate([w2_ref[...], jnp.zeros((hid, LANES - classes), F32)], axis=1).astype(BF16)
+        w2p[:, 0:LANES] = wide
+        w2p[:, LANES:2 * LANES] = wide
+    with scope('countx'):
+        next(count)
+
+    with scope('own'):
+        for i in range(n_chunks):
+            s = slice(i * chunk, (i + 1) * chunk)
+            z2own[s, :] = (mm(h1t[s, :], at[0, 0:n, :], 1, 0) + mm(h1t[s, :], at[1, 0:n, :], 1, 0)
+                           + mm(h1t[s, :], at[2, 0:n, :], 1, 0))
+            if i == 0:
+                for _ in rounds:
+                    pass
+                next(count)
+    with scope('z2wait'):
+        arrived(ops)
+    with scope('z2'):
+        z1h = three(hr[1][:, 0:kf].astype(BF16))
+        logits = jnp.zeros((LANES, n), F32)
+        for i in range(n_chunks):
+            s = slice(i * chunk, (i + 1) * chunk)
+            h1h[s, :] = jnp.maximum(mm(w1p[:, s], z1h, 0, 1), 0.0).astype(BF16)
+            z2 = (z2own[s, :] + mm(h1h[s, :], ath[...], 1, 0)).astype(BF16)
+            z2t[s, :] = z2
+            logits = logits + mm(w2p[s, 0:LANES], z2, 0, 0)
+    with scope('countwait'):
+        for _ in count:
+            pass
+
+    with scope('softmax'):
+        loaded('lab')
+        label_count = mb[4, 0:1, 0:1]
+        ids = lax.broadcasted_iota(jnp.int32, (LANES, n), 0)
+        valid = ids < classes
+        top = jnp.max(jnp.where(valid, logits, -jnp.inf), axis=0, keepdims=True)
+        log_norm = jnp.log(jnp.sum(jnp.where(valid, jnp.exp(logits - top), 0.0), axis=0, keepdims=True)) + top
+        onehot = ids == lab_ref[...]
+        picked = jnp.sum(jnp.where(onehot, logits, 0.0), axis=0, keepdims=True)
+        loss = jnp.sum(weight * (log_norm - picked))
+        prob = jnp.exp(logits - log_norm)
+        scale = weight / label_count
+        gt = jnp.where(valid, (prob - onehot.astype(F32)) * scale, 0.0).astype(BF16)
+        back = mm(ath[...], gt, 1, 1)
+        ops = exchange(2, back[0:halo] + back[halo:2 * halo] + back[2 * halo:3 * halo])
+
+    with scope('grad2'):
+        b2 = refs2[0]
+        lane = lax.broadcasted_iota(jnp.int32, (chunk, LANES), 1)
+        for i in range(n_chunks):
+            s = slice(i * chunk, (i + 1) * chunk)
+            b2[s, :] = jnp.where(lane == classes, loss, mm(z2t[s, :], gt, 1, 1))
+        stream2 = Stream(g, refs2, hid).steps()
+        next(stream2)
+
+    with scope('ptown'):
+        pt = mm(gt, at[0, 0:n, :], 1, 1) + mm(gt, at[1, 0:n, :], 1, 1) + mm(gt, at[2, 0:n, :], 1, 1)
+    with scope('s2core'):
+        next(stream2)
+    with scope('ptwait'):
+        arrived(ops)
+    with scope('dh'):
+        pt = pt + mm(jnp.concatenate(split3(hr[2]), axis=0), sel[...], 0, 0)
+        for j, part in enumerate(split3(pt)):
+            ptc[j * LANES:(j + 1) * LANES, :] = part
+        for i in range(n_chunks):
+            s = slice(i * chunk, (i + 1) * chunk)
+            dh = mm(w2p[s, :], ptc[0:2 * LANES, :], 1, 0) + mm(w2p[s, 0:LANES], ptc[2 * LANES:3 * LANES, :], 1, 0)
+            d1t[s, :] = jnp.where(h1t[s, :].astype(F32) > 0.0, dh, 0.0).astype(BF16)
+    with scope('grad1'):
+        b1 = refs1[0]
+        half = hid // 2
+        b1[...] = mm(d1t[0:half, :], z1t[...], 1, 1) + mm(d1t[half:hid, :], z1tb[...], 1, 1)
+        stream1 = Stream(g, refs1, half).steps()
+        next(stream1)
+    active = [(2, stream2), (1, stream1)]
+    k = 0
     while active:
-        for stream in list(active):
-            if next(stream, 'end') == 'end':
-                active.remove(stream)
-
-    f2, f1 = refs2[8], refs1[8]
-    loss_ref[...] = f2[0:1, classes:classes + 1] / label_count
-    g2_ref[...] = f2[:, 0:classes]
-    flip = jnp.transpose(f1[...])
-    g1_ref[:, 0:half] = flip[0:feat_in, :]
-    g1_ref[:, half:hid] = flip[LANES // 2:LANES // 2 + feat_in, :]
+        for which, stream in list(active):
+            k += 1
+            with scope('sum%d_%d' % (which, k)):
+                if next(stream, 'end') == 'end':
+                    active.remove((which, stream))
+
+    with scope('out'):
+        f2, f1 = refs2[8], refs1[8]
+        loss_ref[...] = f2[0:1, classes:classes + 1] / label_count
+        g2_ref[...] = f2[:, 0:classes]
+        flip = jnp.transpose(f1[...])
+        g1_ref[:, 0:half] = flip[0:feat_in, :]
+        g1_ref[:, half:hid] = flip[LANES // 2:LANES // 2 + feat_in, :]
 
 
 def stream_scratch(rows, dims):
@@ -367,28 +424,35 @@
         hid, classes = w_two.shape
         halo = send_rows.size
         ext = n + halo
+        deg = edge_src.shape[1]
         nx, ny, nz, nc = dims
         n_count = nx + ny + nz + nc - 4
         kf = 64
         scratch = [
-            pltpu.VMEM((3, ext, n), BF16), pltpu.VMEM((LANES, n), BF16), pltpu.VMEM((kf, hid), BF16), pltpu.VMEM((hid, LANES), BF16),
-            pltpu.VMEM((halo, n), BF16), pltpu.VMEM((LANES, n), BF16), pltpu.VMEM((LANES, n), BF16),
-            pltpu.VMEM((hid, n), BF16), pltpu.VMEM((hid, halo), BF16), pltpu.VMEM((hid, n), BF16),
-            pltpu.VMEM((hid, n), BF16), pltpu.VMEM((3, LANES, n), BF16),
+            pltpu.VMEM((feat_in, n), BF16), pltpu.VMEM((feat_in, hid), F32), pltpu.VMEM((hid, classes), F32),
+            pltpu.VMEM(send_rows.shape, jnp.int32), pltpu.VMEM((deg, n), jnp.int32), pltpu.VMEM((deg, n), F32),
+            pltpu.VMEM((1, n), jnp.int32), pltpu.VMEM((1, n), jnp.int32), pltpu.SemaphoreType.DMA((8,)),
+            pltpu.VMEM((3, ext, n), BF16), pltpu.VMEM((3 * halo, n), BF16), pltpu.VMEM((LANES, n), BF16),
+            pltpu.VMEM((kf, hid), BF16), pltpu.VMEM((hid, 2 * LANES), BF16), pltpu.VMEM((3 * halo, n), BF16),
+            pltpu.VMEM((LANES, n), BF16), pltpu.VMEM((LANES, n), BF16),
+            pltpu.VMEM((hid, n), BF16), pltpu.VMEM((hid, 3 * halo), BF16), pltpu.VMEM((hid, n), F32),
+            pltpu.VMEM((hid, n), BF16), pltpu.VMEM((hid, n), BF16), pltpu.VMEM((3 * LANES, n), BF16),
             pltpu.VMEM((3, halo, LANES), F32), pltpu.VMEM((3, halo, LANES), F32),
             pltpu.SemaphoreType.DMA((3, PEERS)), pltpu.SemaphoreType.DMA((3, PEERS)),
             pltpu.VMEM((5, 8, LANES), F32), pltpu.VMEM((n_count, 8, LANES), F32),
             pltpu.SemaphoreType.DMA((n_count,)), pltpu.SemaphoreType.DMA((n_count,)),
+            pltpu.SemaphoreType.REGULAR((max(nz // 2 - 1, 1),)),
         ] + stream_scratch(hid, dims) + stream_scratch(hid // 2, dims)
         vmem = pl.BlockSpec(memory_space=pltpu.VMEM)
         loss, grad_one, grad_two = pl.pallas_call(
             functools.partial(step_kernel, dims, feat_in, classes),
             out_shape=(jax.ShapeDtypeStruct((1, 1), F32), jax.ShapeDtypeStruct((feat_in, hid), F32),
                        jax.ShapeDtypeStruct((hid, classes), F32)),
-            in_specs=[vmem] * 8, out_specs=(vmem,) * 3, scratch_shapes=scratch,
+            in_specs=[pl.BlockSpec(memory_space=pltpu.HBM)] * 8, out_specs=(vmem,) * 3, scratch_shapes=scratch,
             compiler_params=pltpu.CompilerParams(collective_id=0, has_side_effects=True,
-                                                 vmem_limit_bytes=60 * 1024 * 1024),
-        )(node_feat.T, w_one, w_two, send_rows, edge_src.T, edge_wt.T, labels.reshape(1, n), label_mask.reshape(1, n))
+                                                 vmem_limit_bytes=32 * 1024 * 1024),
+        )(*[pltpu.with_memory_space_constraint(v, pltpu.HBM) for v in (
+            node_feat.T, w_one, w_two, send_rows, edge_src.T, edge_wt.T, labels.reshape(1, n), label_mask.reshape(1, n))])
         return loss[0, 0], grad_one, grad_two
     return device_step
 

time: 79.9 us -> 66.4 us (0.83)
  Pallas kernels: 73.2 us -> 62.2 us
  local copies, waits for them, and re-layouts: 4.08 us -> 1.74 us
    pallas_call x1, Pallas kernels: 73.2 us -> 62.2 us  [device_step(): pl.pallas_call(functools.partial(step_kernel, dims, feat_in, classes), ou...]
    unnamed x2, local copies, waits for them, and re-layouts: 4.08 us -> 1.74 us
where the time goes in v2:
time: 66.4 us; the launch traced here: 66.2 us
  Pallas kernels  62.2 us (94%)
  between operations  2.33 us (4%)
  local copies, waits for them, and re-layouts  1.74 us (3%)
    pallas_call x1, Pallas kernels, device_step(): pl.pallas_call(functools.partial(step_kernel, dims, feat_in, classes), ou...  62.2 us
    unnamed x2, local copies, waits for them, and re-layouts  1.74 us

profile of v2, /device:TPU:1, one launch (start us, length us, event | category | flops | bytes accessed | tf_op | source)
XLA Modules:
  0.0 66.2 jit_solution(9395314451691522697)
XLA Ops:
  0.6 62.2 %shard_map.103 = (f32[1,1]{1,0:T(1,128)}, f32[50,2048]{1,0:T(8,128)S(1)}, f32[2048,121]{1,0:T(8,128)S(1)}) custom-call(bf16[50,512]{1,0:T(8,128)(2,1)} %bitcast.6, f32[50,2048]{1,0:T(8,128)} %w1_hbm.1, f32[2048,121]{1,0:T(8,128)} %w2_hbm.1, s32[4,8]{1,0:T(4,128)} %send_hbm.1, s32[12,512]{1,0:T(8,128)} %bitcast.7, f32[12,512]{1,0:T(8,128)} %bitcast.8, ...), custom_call_target="tpu_custom_call" | custom-call | tf_op jit(solution)/shard_map/pallas_call | solution.py:447
  63.4 0.8 %copy.15 = f32[50,2048]{1,0:T(8,128)} copy(f32[50,2048]{1,0:T(8,128)S(1)} %get-tuple-element.13) | data formatting | bytes 819200
  64.1 1.0 %copy.16 = f32[2048,121]{1,0:T(8,128)} copy(f32[2048,121]{1,0:T(8,128)S(1)} %get-tuple-element.14) | data formatting | bytes 1982464
